TPU v7x, 256 devices: a whole 4x4x8 slice. The times are simulated.
256 devices in a mesh: req: 64 (over x, y, z_hi), mesh: 4 (over z_lo, core).
Axes of the slice: x: 4, y: 4, z: 8 (z_hi: 4, z_lo: 2; z = z_hi * 2 + z_lo), core: 2. Of those that a mesh axis runs over, the one named last changes fastest.
Arguments:
- tokens: bfloat16 [1024, 64, 1024], P(('req', 'mesh')), may hold values from -6 to 6
- lengths: int32 [1024], P(('req', 'mesh')), may hold values from 1 to 64, 49152 in all
- ridge_keys: float32 [1024, 8, 128, 128], P(('req', 'mesh')), as said below
- ridge_values: float32 [1024, 8, 128, 128], P(('req', 'mesh')), may hold values from -0.5 to 0.5
- conv_tail: bfloat16 [1024, 3, 3072], P(('req', 'mesh')), may hold values from -6 to 6
- page_table: int32 [1024], P(('req', 'mesh')), may hold values from 0 to 15, as said below
- w_qkv: bfloat16 [1024, 3072], P(('req', 'mesh')), may hold values from -0.1875 to 0.1875
- conv_weight: float32 [4, 3072], replicated, may hold values from -3 to 3
- w_gates: bfloat16 [1024, 16], replicated, may hold values from -0.1875 to 0.1875
- decay_rate: float32 [8], replicated, may hold values from 0.001 to 0.03
- ridge: float32 [8], replicated, may hold values from 0.01 to 0.1
- w_out: bfloat16 [1024, 1024], P(('req', 'mesh')), may hold values from -0.1875 to 0.1875
- attn_gain: float32 [1024], replicated, may hold values from 0.5 to 1.5
- ffn_gain: float32 [1024], replicated, may hold values from 0.5 to 1.5
- w_gate: bfloat16 [1024, 2816], P('req', 'mesh'), may hold values from -0.1875 to 0.1875
- w_up: bfloat16 [1024, 2816], P('req', 'mesh'), may hold values from -0.1875 to 0.1875
- w_down: bfloat16 [2816, 1024], P('mesh', 'req'), may hold values from -0.109375 to 0.109375
Outputs:
- mixed: bfloat16 [1024, 64, 1024], P(('req', 'mesh'))
- keys_decode: float32 [1024, 8, 128, 128], P(('req', 'mesh'))
- values_decode: float32 [1024, 8, 128, 128], P(('req', 'mesh'))
- tail_decode: bfloat16 [1024, 3, 3072], P(('req', 'mesh'))
- readout: bfloat16 [1024, 64, 1024], P(('req', 'mesh'))
Inputs may be any that keep to these rules, and one draw needn't show every extreme that they name: `page_table`: within each group of 16 consecutive requests the values are a permutation; value // 4 is a decode device of the group and value % 4 a slot on it, and the 4 requests of one device go to 4 different decode devices. `ridge_keys`: each matrix is symmetric with a positive diagonal that exceeds the sum of the magnitudes of its row's other entries.
All inputs are finite; a program needn't handle non-finite values. No bound on the sum of `lengths` on one device may be relied on, other than what follows from the above.
Results may differ from a plain program's by a relative error of at most 0.0095.
Values may be sent and summed in bfloat16 or wider, within the bound.
A program may use at most 128 MiB of HBM per device.

v0:
```python
import jax
import jax.numpy as jnp
from jax import lax
from jax.sharding import PartitionSpec as P

ITERS = 5


def rms_norm(values, gain):
    return values * lax.rsqrt(jnp.mean(values * values, axis=-1, keepdims=True) + 1e-05) * gain


def unit_rows(values):
    return values * lax.rsqrt(jnp.sum(values * values, axis=-1, keepdims=True) + 1e-06)


def prepare_heads(projected, gate_logits, conv_tail, lengths, conv_weight, decay_rate):
    requests, length, columns = projected.shape
    heads = decay_rate.shape[0]
    window = conv_tail.shape[1]
    extended = jnp.concatenate([conv_tail, projected], axis=1)
    conv_sum = jnp.zeros((requests, length, columns), jnp.float32)
    for tap_index in range(window + 1):
        conv_sum = conv_sum + conv_weight[tap_index] * extended[
            :, tap_index : tap_index + length
        ].astype(jnp.float32)
    activated = jax.nn.silu(conv_sum).reshape(requests, length, 3, heads, columns // (3 * heads))
    queries = unit_rows(activated[:, :, 0])
    keys_now = unit_rows(activated[:, :, 1])
    values_now = activated[:, :, 2]
    position = jnp.arange(length, dtype=jnp.int32)
    live = (position[None, :] < lengths[:, None]).astype(jnp.float32)[:, :, None]
    beta = jax.nn.sigmoid(gate_logits[..., 0]) * live
    log_decay = -decay_rate * jax.nn.softplus(gate_logits[..., 1]) * live
    new_tail = jax.vmap(
        lambda rows_all, first_row: lax.dynamic_slice_in_dim(rows_all, first_row, window, 0)
    )(extended, lengths)
    return (queries, keys_now, values_now, beta, log_decay, new_tail)


def mesa_core(
    queries, keys_now, values_now, beta, log_decay, keys_start, values_start, ridge, iterations
):
    highest = lax.Precision.HIGHEST
    cumulative = jnp.cumsum(jnp.swapaxes(log_decay, 1, 2), axis=-1)
    beta_heads = jnp.swapaxes(beta, 1, 2)
    length = cumulative.shape[-1]
    position = jnp.arange(length, dtype=jnp.int32)
    causal = position[:, None] >= position[None, :]
    spread = cumulative[..., :, None] - cumulative[..., None, :]
    weight = jnp.where(causal, jnp.exp(jnp.minimum(spread, 0.0)), 0.0) * beta_heads[..., None, :]
    carried = jnp.swapaxes(jnp.exp(cumulative), 1, 2)[..., None]
    ridge_term = ridge[None, None, :, None]
    solution = jnp.zeros_like(queries)
    residual = queries
    direction = queries
    res_norm = jnp.sum(residual * residual, axis=-1, keepdims=True)
    for step_index in range(iterations):
        start_part = carried * jnp.einsum(
            "bthj,bhij->bthi", direction, keys_start, precision=highest
        )
        apply_scores = (
            jnp.einsum("bthj,bshj->bhts", direction, keys_now, precision=highest) * weight
        )
        applied = (
            start_part
            + jnp.einsum("bhts,bshj->bthj", apply_scores, keys_now, precision=highest)
            + ridge_term * direction
        )
        step_size = res_norm / (jnp.sum(direction * applied, axis=-1, keepdims=True) + 1e-20)
        solution = solution + step_size * direction
        residual = residual - step_size * applied
        next_norm = jnp.sum(residual * residual, axis=-1, keepdims=True)
        direction = residual + next_norm / (res_norm + 1e-20) * direction
        res_norm = next_norm
    read_start = carried * jnp.einsum("bthj,bhij->bthi", solution, values_start, precision=highest)
    scores = jnp.einsum("bthj,bshj->bhts", solution, keys_now, precision=highest) * weight
    readout = read_start + jnp.einsum("bhts,bshj->bthj", scores, values_now, precision=highest)
    tail_weight = jnp.swapaxes(jnp.exp(cumulative[..., -1:] - cumulative) * beta_heads, 1, 2)[
        ..., None
    ]
    final_decay = jnp.exp(cumulative[..., -1])[..., None, None]
    keys_end = final_decay * keys_start + jnp.einsum(
        "bshi,bshj->bhij", keys_now * tail_weight, keys_now, precision=highest
    )
    values_end = final_decay * values_start + jnp.einsum(
        "bshi,bshj->bhij", values_now * tail_weight, keys_now, precision=highest
    )
    return (readout, keys_end, values_end)


def shards(
    tokens,
    lengths,
    ridge_keys,
    ridge_values,
    conv_tail,
    page_table,
    w_qkv,
    conv_weight,
    w_gates,
    decay_rate,
    ridge,
    w_out,
    attn_gain,
    ffn_gain,
    w_gate,
    w_up,
    w_down,
):
    highest = lax.Precision.HIGHEST
    requests, length, width = tokens.shape
    heads = decay_rate.shape[0]
    row_count = requests * length
    resident = tokens.astype(jnp.float32).reshape(row_count, width)
    normed = rms_norm(resident, attn_gain).astype(jnp.bfloat16)
    columns_in = normed
    projected = jnp.dot(
        columns_in,
        lax.all_gather(w_qkv, ("req", "mesh"), axis=0, tiled=True),
        preferred_element_type=jnp.float32,
    )
    projected = projected.astype(jnp.bfloat16).reshape(requests, length, -1)
    gate_logits = jnp.dot(normed, w_gates, preferred_element_type=jnp.float32).reshape(
        requests, length, heads, 2
    )
    queries, keys_now, values_now, beta, log_decay, new_tail = prepare_heads(
        projected, gate_logits, conv_tail, lengths, conv_weight, decay_rate
    )
    readout, keys_end, values_end = mesa_core(
        queries, keys_now, values_now, beta, log_decay, ridge_keys, ridge_values, ridge, ITERS
    )
    head_rows = readout.reshape(row_count, -1).astype(jnp.bfloat16)
    columns_in = head_rows
    attended = jnp.dot(
        columns_in,
        lax.all_gather(w_out, ("req", "mesh"), axis=0, tiled=True),
        preferred_element_type=jnp.float32,
    )
    after_attn = (resident + attended).astype(jnp.bfloat16)
    ffn_in = rms_norm(after_attn.astype(jnp.float32), ffn_gain).astype(jnp.bfloat16)
    group_tokens = lax.all_gather(ffn_in, "mesh", axis=0, tiled=True)
    columns_in = group_tokens
    gate_proj = jnp.dot(
        columns_in,
        lax.all_gather(w_gate, "req", axis=0, tiled=True),
        preferred_element_type=jnp.float32,
    )
    upward = jnp.dot(
        columns_in,
        lax.all_gather(w_up, "req", axis=0, tiled=True),
        preferred_element_type=jnp.float32,
    )
    hidden = (jax.nn.silu(gate_proj) * upward).astype(jnp.bfloat16)
    down_whole = lax.all_gather(w_down, "req", axis=1, tiled=True)
    ffn_out = lax.psum_scatter(
        jnp.dot(hidden, down_whole, preferred_element_type=jnp.float32).astype(jnp.bfloat16),
        "mesh",
        scatter_dimension=0,
        tiled=True,
    ).astype(jnp.float32)
    mixed = (
        (after_attn.astype(jnp.float32) + ffn_out)
        .astype(jnp.bfloat16)
        .reshape(requests, length, width)
    )
    peers = lax.axis_size("mesh")
    destination = page_table // requests
    slot_index = page_table % requests
    select = (destination[None, :] == jnp.arange(peers, dtype=jnp.int32)[:, None]).astype(
        jnp.float32
    )
    send_keys = jnp.einsum("ej,jhab->ehab", select, keys_end, precision=highest)
    send_values = jnp.einsum("ej,jhab->ehab", select, values_end, precision=highest)
    send_tail = jnp.einsum(
        "ej,jrc->erc", select, new_tail.astype(jnp.float32), precision=highest
    ).astype(jnp.bfloat16)
    send_slot = jnp.sum(jnp.where(select > 0.5, slot_index[None, :], 0), axis=1)
    got_keys, got_values, got_tail, got_slot = (
        lax.all_to_all(
            send_keys.astype(jnp.bfloat16), "mesh", split_axis=0, concat_axis=0, tiled=True
        ).astype(send_keys.dtype),
        lax.all_to_all(
            send_values.astype(jnp.bfloat16), "mesh", split_axis=0, concat_axis=0, tiled=True
        ).astype(send_values.dtype),
        lax.all_to_all(send_tail, "mesh", split_axis=0, concat_axis=0, tiled=True),
        lax.all_to_all(send_slot, "mesh", split_axis=0, concat_axis=0, tiled=True),
    )
    placing = (got_slot[None, :] == jnp.arange(requests, dtype=jnp.int32)[:, None]).astype(
        jnp.float32
    )
    keys_decode = jnp.einsum("si,ihab->shab", placing, got_keys, precision=highest)
    values_decode = jnp.einsum("si,ihab->shab", placing, got_values, precision=highest)
    tail_decode = jnp.einsum(
        "si,irc->src", placing, got_tail.astype(jnp.float32), precision=highest
    ).astype(jnp.bfloat16)
    return (mixed, keys_decode, values_decode, tail_decode, head_rows.reshape(requests, length, -1))


def solution(mesh):
    in_specs = (
        P(("req", "mesh"), None, None),
        P(("req", "mesh")),
        P(("req", "mesh"), None, None, None),
        P(("req", "mesh"), None, None, None),
        P(("req", "mesh"), None, None),
        P(("req", "mesh")),
        P(("req", "mesh"), None),
        P(),
        P(),
        P(),
        P(),
        P(("req", "mesh"), None),
        P(),
        P(),
        P("req", "mesh"),
        P("req", "mesh"),
        P("mesh", "req"),
    )
    out_specs = (
        P(("req", "mesh"), None, None),
        P(("req", "mesh"), None, None, None),
        P(("req", "mesh"), None, None, None),
        P(("req", "mesh"), None, None),
        P(("req", "mesh"), None, None),
    )
    return jax.shard_map(shards, mesh=mesh, in_specs=in_specs, out_specs=out_specs, check_vma=False)
```

profile of v0, /device:TPU:1, one launch (start us, length us, event | category | flops | bytes accessed | tf_op | source)
XLA Modules:
  0.0 583.6 jit_solution(5874164278874121975)
XLA Ops:
  17.6 102.5 %all-gather.19.cloned.1.call-done = bf16[256,4,1024]{2,1,0:T(4,128)(2,1)} async-done(((bf16[1,4,1024]{2,1,0:T(4,128)(2,1)}), bf16[256,4,1024]{2,1,0:T(4,128)(2,1)}) %all-gather.19.cloned.1.call-update) | async-done | bytes 2097168 | tf_op jit(solution)/shard_map/all_gather | solution.py:137
  120.0 3.9 reshape.219
  124.0 114.9 %all-gather.17.cloned.1.call-done = bf16[256,4,3072]{2,1,0:T(4,128)(2,1)} async-done(((bf16[1,4,3072]{2,1,0:T(4,128)(2,1)}), bf16[256,4,3072]{2,1,0:T(4,128)(2,1)}) %all-gather.17.cloned.1.call-update) | async-done | bytes 6291472 | tf_op jit(solution)/shard_map/all_gather | solution.py:120
  238.8 10.7 %reshape.217 = bf16[1024,3072]{1,0:T(8,128)(2,1)} reshape(bf16[256,4,3072]{2,1,0:T(4,128)(2,1)} %all-gather.17.cloned.1.call-done) | data formatting | bytes 12582912
  249.5 4.6 convolution_convert_fusion
  254.1 2.2 divide_multiply_fusion
  259.2 4.1 fusion.30
  263.3 2.2 convolution_multiply_fusion.5
  265.5 2.1 multiply_reduce_fusion.7
  268.7 1.5 multiply_add_fusion.6
  270.2 2.0 convolution_multiply_fusion.4
  272.2 4.1 fusion.27
  276.4 1.7 multiply_reduce_fusion.5
  278.1 1.5 multiply_reduce_fusion.4
  280.0 2.0 convolution_multiply_fusion.3
  282.0 4.1 fusion.24
  286.1 1.7 multiply_reduce_fusion.3
  288.9 2.0 convolution_multiply_fusion.2
  290.9 4.3 fusion.21
  295.3 1.7 multiply_reduce_fusion.1
  298.4 4.1 fusion.18
  302.6 2.0 convolution_multiply_fusion.1
  304.6 1.6 fusion.34
  306.2 2.4 multiply_add_fusion.2
  308.6 2.0 convolution_multiply_fusion
  310.6 4.2 fusion.15
  321.2 3.4 all-to-all-start
  324.8 1.9 pad_maximum_fusion
  326.7 2.5 copy.96
  329.1 1.6 gather_fusion
  330.8 17.8 %all-gather.9.cloned.1.call-done = bf16[1024,1024]{1,0:T(8,128)(2,1)} async-done(((bf16[256,1024]{1,0:T(8,128)(2,1)}), bf16[1024,1024]{1,0:T(8,128)(2,1)}) %all-gather.9.cloned.1.call-update) | async-done | bytes 2097168 | tf_op jit(solution)/shard_map/all_gather | solution.py:142
  348.6 5.3 fusion.107
  353.9 73.4 %all-gather.13.cloned.1.call-done = bf16[1024,704]{1,0:T(8,128)(2,1)} async-done(((bf16[16,704]{1,0:T(8,128)(2,1)}), bf16[1024,704]{1,0:T(8,128)(2,1)}) %all-gather.13.cloned.1.call-update) | async-done | bytes 1441808 | tf_op jit(solution)/shard_map/all_gather | solution.py:151
  427.3 77.3 %all-gather.15.cloned.1.call-done = bf16[704,1024]{0,1:T(8,128)(2,1)} async-done(((bf16[704,16]{0,1:T(8,128)(2,1)}), bf16[704,1024]{0,1:T(8,128)(2,1)}) %all-gather.15.cloned.1.call-update) | async-done | bytes 1441808 | tf_op jit(solution)/shard_map/all_gather | solution.py:155
  504.6 8.2 %convolution_convert_fusion.3 = bf16[1024,1024]{1,0:T(8,128)(2,1)} fusion(bf16[704,1024]{0,1:T(8,128)(2,1)} %all-gather.15.cloned.1.call-done, f32[1024,704]{0,1:T(8,128)} %fusion.107, bf16[1024,1024]{1,0:T(8,128)(2,1)} %all-gather.9.cloned.1.call-done, bf16[1024,704]{1,0:T(8,128)(2,1)} %all-gather.13.cloned.1.call-done), kind=kOutput, calls=%fused_computation.16 | convolution fusion | flops 2958163968 | bytes 9961472 | tf_op jit(solution)/shard_map/dot_general | solution.py:157
  513.7 7.5 %multiply_add_fusion = f32[4,8,128,128]{3,2,1,0:T(8,128)} fusion(f32[4,8,128,128]{3,2,1,0:T(8,128)} %param.20, f32[4,8]{1,0:T(4,128)S(1)} %exp.47, f32[4,64,1,8,128]{4,3,2,1,0:T(8,128)} %copy-done.1, f32[4,64,8]{1,2,0:T(8,128)S(1)} %get-tuple-element.43, f32[4,64,1,8,128]{4,3,2,1,0:T(8,128)S(1)} %get-tuple-element.37, f32[4,64,8]{1,2,0:T(8,128)S(1)} %add_rsqrt_fusion), kind=kOutput, calls=%fused_computation.14 | convolution fusion | flops 404226048 | bytes 6307968 | tf_op jit(solution)/shard_map/bshi,bshj->bhij/dot_general | solution.py:86
  521.1 4.8 all-to-all-start.3
  525.9 4.9 fusion.11
  532.0 4.2 all-to-all-start.2
  536.3 4.7 multiply_add_fusion.1
  541.0 3.3 fusion.8
  545.5 8.5 %all-to-all-done.2 = bf16[4,8,128,128]{3,2,1,0:T(8,128)(2,1)} async-done(((bf16[4,8,128,128]{3,2,1,0:T(8,128)(2,1)}), bf16[4,8,128,128]{3,2,1,0:T(8,128)(2,1)}, u32[]{:S(2)}, u32[]{:S(2)}) %all-to-all-start.2) | async-done | bytes 1048608 | tf_op jit(solution)/shard_map/all_to_all | solution.py:183
  554.0 4.3 all-to-all-start.1
  560.1 2.1 fusion.41
  562.2 1.6 copy.101
  563.8 8.0 %all-to-all-done.1 = bf16[4,8,128,128]{3,2,1,0:T(8,128)(2,1)S(1)} async-done(((bf16[4,8,128,128]{3,2,1,0:T(8,128)(2,1)}), bf16[4,8,128,128]{3,2,1,0:T(8,128)(2,1)S(1)}, u32[]{:S(2)}, u32[]{:S(2)}) %all-to-all-start.1) | async-done | bytes 1048608 | tf_op jit(solution)/shard_map/all_to_all | solution.py:180
  572.7 1.6 copy.100
  574.3 2.0 fusion.38
  (104 shorter events, 29.5 us)
Async XLA Ops:
  7.2 9.4 %copy-start.8 = (bf16[4,64,1024]{2,1,0:T(8,128)(2,1)S(1)}, bf16[4,64,1024]{2,1,0:T(8,128)(2,1)}, u32[]{:S(2)}) copy-start(bf16[4,64,1024]{2,1,0:T(8,128)(2,1)} %param.17) | copy-start | bytes 1572868
  7.2 10.2 %copy-start.11 = (bf16[4,3,3072]{2,0,1:T(4,128)(2,1)S(1)}, bf16[4,3,3072]{2,0,1:T(4,128)(2,1)}, u32[]{:S(2)}) copy-start(bf16[4,3,3072]{2,0,1:T(4,128)(2,1)} %param.21) | copy-start | bytes 221188
  7.2 112.8 %all-gather.19.cloned.1.call-start = ((), (), s32[]{:S(2)}) async-start(), calls=%async_computation.11 | async-start | bytes 2105344 | tf_op jit(solution)/shard_map/all_gather | solution.py:137
  7.9 230.9 %all-gather.17.cloned.1.call-start = ((), (), s32[]{:S(2)}) async-start(), calls=%async_computation.10 | async-start | bytes 6316032 | tf_op jit(solution)/shard_map/all_gather | solution.py:120
  8.7 322.1 %all-gather.11.cloned.1.call-start = ((), (), s32[]{:S(2)}) async-start(), calls=%async_computation.6 | async-start | bytes 1597440 | tf_op jit(solution)/shard_map/all_gather | solution.py:146
  9.4 339.2 %all-gather.9.cloned.1.call-start = ((), (), s32[]{:S(2)}) async-start(), calls=%async_computation.5 | async-start | bytes 2621440 | tf_op jit(solution)/shard_map/all_gather | solution.py:142
  254.1 2.3 copy-start.3
  257.2 57.6 %copy-start.1 = (f32[4,64,1,8,128]{4,3,2,1,0:T(8,128)}, f32[4,64,1,8,128]{4,3,2,1,0:T(8,128)S(1)}, u32[]{:S(2)}) copy-start(f32[4,64,1,8,128]{4,3,2,1,0:T(8,128)S(1)} %get-tuple-element.36) | copy-start | bytes 3145732
  257.2 2.0 copy-start
  263.3 2.2 copy-start.12
  308.5 2.0 copy-start.2
  314.8 1.7 copy-start.9
  314.8 1.8 copy-start.10
  316.1 1.3 copy-start.4
  316.5 1.6 copy-start.13
  316.5 3.8 copy-start.15
  316.5 8.2 %copy-start.14 = (s32[4]{0:T(128)S(1)}, s32[4]{0:T(128)}, u32[]{:S(2)}) copy-start(s32[4]{0:T(128)} %param.18) | copy-start | bytes 52
  317.4 0.8 copy-start.6
  319.2 108.1 %all-gather.13.cloned.1.call-start = ((), (), s32[]{:S(2)}) async-start(), calls=%async_computation.7 | async-start | bytes 1597440 | tf_op jit(solution)/shard_map/all_gather | solution.py:151
  319.8 184.8 %all-gather.15.cloned.1.call-start = ((), (), s32[]{:S(2)}) async-start(), calls=%async_computation.8 | async-start | bytes 1597440 | tf_op jit(solution)/shard_map/all_gather | solution.py:155
  321.2 199.9 %all-to-all-start = ((s32[4,1,1]{2,1,0:T(1,128)}), s32[4,1,1]{2,1,0:T(1,128)S(1)}, u32[]{:S(2)}, u32[]{:S(2)}) async-start(s32[4,1,1]{2,1,0:T(1,128)} %copy.89), calls=%async_computation.1 | async-start | bytes 4096 | tf_op jit(solution)/shard_map/all_to_all | solution.py:187
  324.6 249.7 %reduce-scatter.2.cloned.1.call-start = ((), (), s32[]{:S(2)}) async-start(), calls=%async_computation.9 | async-start | bytes 2621440 | tf_op jit(solution)/shard_map/reduce_scatter | solution.py:156
  521.1 10.9 %all-to-all-start.3 = ((bf16[4,3,3072]{2,1,0:T(4,128)(2,1)}), bf16[4,3,3072]{2,1,0:T(4,128)(2,1)S(1)}, u32[]{:S(2)}, u32[]{:S(2)}) async-start(bf16[4,3,3072]{2,1,0:T(4,128)(2,1)} %copy.97), calls=%async_computation.4 | async-start | bytes 196608 | tf_op jit(solution)/shard_map/all_to_all | solution.py:186
  532.0 22.0 %all-to-all-start.2 = ((bf16[4,8,128,128]{3,2,1,0:T(8,128)(2,1)}), bf16[4,8,128,128]{3,2,1,0:T(8,128)(2,1)}, u32[]{:S(2)}, u32[]{:S(2)}) async-start(bf16[4,8,128,128]{3,2,1,0:T(8,128)(2,1)} %copy.94), calls=%async_computation.3 | async-start | bytes 2097152 | tf_op jit(solution)/shard_map/all_to_all | solution.py:183
  544.3 14.1 %copy-start.5 = (bf16[4,64,8,128]{3,1,2,0:T(8,128)(2,1)S(1)}, bf16[4,64,8,128]{3,1,2,0:T(8,128)(2,1)}, u32[]{:S(2)}) copy-start(bf16[4,64,8,128]{3,1,2,0:T(8,128)(2,1)} %copy-done.4) | copy-start | bytes 1572868
  554.0 17.8 %all-to-all-start.1 = ((bf16[4,8,128,128]{3,2,1,0:T(8,128)(2,1)}), bf16[4,8,128,128]{3,2,1,0:T(8,128)(2,1)S(1)}, u32[]{:S(2)}, u32[]{:S(2)}) async-start(bf16[4,8,128,128]{3,2,1,0:T(8,128)(2,1)} %copy.91), calls=%async_computation.2 | async-start | bytes 2097152 | tf_op jit(solution)/shard_map/all_to_all | solution.py:180
  572.7 1.6 copy-start.7
Sparse Core Ops, SparseCore 0:
  11.8 108.2 all-gather.18
  123.9 114.9 all-gather.16
  242.1 72.7 all-gather.10
  319.3 29.2 all-gather.8
  351.7 75.5 all-gather.12
  430.4 74.1 all-gather.14
  512.9 34.4 reduce-scatter.1
where the time goes:
time: 594 us; the launch traced here: 584 us
  waiting for transfers between devices  405 us (68%)
  matrix products  92 us (15%)
  local copies, waits for them, and re-layouts  32 us (5%)
  other arithmetic  21.9 us (4%)
  starting transfers between devices  17.1 us (3%)
  between operations  15.2 us (3%)
    all_gather x1, waiting for transfers between devices, shards(): lax.all_gather(w_qkv, ('req', 'mesh'), axis=0, tiled=True)  115 us
    all_gather x1, waiting for transfers between devices, shards(): lax.all_gather(w_out, ('req', 'mesh'), axis=0, tiled=True)  102 us
    all_gather x1, waiting for transfers between devices, shards(): down_whole = lax.all_gather(w_down, 'req', axis=1, tiled=True)  77.3 us
    all_gather x1, waiting for transfers between devices, shards(): lax.all_gather(w_up, 'req', axis=0, tiled=True)  73.4 us
    dot_general x5, matrix products, mesa_core(): jnp.einsum('bthj,bhij->bthi', direction, keys_start, precision=highest)  20.9 us
    unnamed x38, local copies, waits for them, and re-layouts  20.7 us
    all_gather x1, waiting for transfers between devices, shards(): group_tokens = lax.all_gather(ffn_in, 'mesh', axis=0, tiled=True)  17.8 us
  transfers between devices with their start and end apart: 11, of which 7 were waited for; matrix products, arithmetic and copies ran while one was open for 24% of the time, Pallas kernels for 0%

commit v1 on v0

--- a/solution.py
+++ b/solution.py
@@ -117,7 +117,12 @@
     columns_in = normed
     projected = jnp.dot(
         columns_in,
-        lax.all_gather(w_qkv, ("req", "mesh"), axis=0, tiled=True),
+        jnp.concatenate(
+            lax.all_to_all(
+                jnp.stack([w_qkv] * lax.axis_size(("req", "mesh"))), ("req", "mesh"), 0, 0
+            ),
+            axis=0,
+        ),
         preferred_element_type=jnp.float32,
     )
     projected = projected.astype(jnp.bfloat16).reshape(requests, length, -1)

time: 594 us -> 522 us (0.88); the launches traced: 584 us -> 518 us
  waiting for transfers between devices: 405 us -> 324 us
  starting transfers between devices: 17.1 us -> 33.5 us
    all_gather x1 -> x0, waiting for transfers between devices: 115 us -> none  [shards(): lax.all_gather(w_qkv, ('req', 'mesh'), axis=0, tiled=True)]
    all_gather x1, waiting for transfers between devices: 102 us -> 127 us  [shards(): lax.all_gather(w_out, ('req', 'mesh'), axis=0, tiled=True)]
    all_to_all x0 -> x1, starting transfers between devices: none -> 16.5 us  [shards(): lax.all_to_all(jnp.stack([w_qkv] * lax.axis_size(('req', 'mesh'))), ('req...]
    all_to_all x0 -> x1, waiting for transfers between devices: none -> 13.9 us  [shards(): lax.all_to_all(jnp.stack([w_qkv] * lax.axis_size(('req', 'mesh'))), ('req...]
    unnamed x38 -> x45, local copies, waits for them, and re-layouts: 20.7 us -> 9.92 us
    reshape x0 -> x1, local copies, waits for them, and re-layouts: none -> 10.6 us  [shards(): jnp.concatenate(lax.all_to_all(jnp.stack([w_qkv] * lax.axis_size(('req',...]
  transfers between devices with their start and end apart: 11 -> 11, of which waited for: 7 -> 7; matrix products, arithmetic and copies ran while one was open for 24% -> 26% of each run, Pallas kernels for 0% -> 0%
where the time goes in v1:
time: 522 us; the launch traced here: 518 us
  waiting for transfers between devices  324 us (62%)
  matrix products  90.8 us (17%)
  local copies, waits for them, and re-layouts  35.3 us (7%)
  starting transfers between devices  33.5 us (6%)
  other arithmetic  19.3 us (4%)
  between operations  15.1 us (3%)
    all_gather x1, waiting for transfers between devices, shards(): lax.all_gather(w_out, ('req', 'mesh'), axis=0, tiled=True)  127 us
    all_gather x1, waiting for transfers between devices, shards(): down_whole = lax.all_gather(w_down, 'req', axis=1, tiled=True)  77.3 us
    all_gather x1, waiting for transfers between devices, shards(): lax.all_gather(w_up, 'req', axis=0, tiled=True)  73.4 us
    dot_general x5, matrix products, mesa_core(): jnp.einsum('bthj,bhij->bthi', direction, keys_start, precision=highest)  20.9 us
    all_to_all x1, starting transfers between devices, shards(): lax.all_to_all(jnp.stack([w_qkv] * lax.axis_size(('req', 'mesh'))), ('req...  16.5 us
    all_to_all x1, waiting for transfers between devices, shards(): lax.all_to_all(jnp.stack([w_qkv] * lax.axis_size(('req', 'mesh'))), ('req...  13.9 us
    all_gather x1, waiting for transfers between devices, shards(): group_tokens = lax.all_gather(ffn_in, 'mesh', axis=0, tiled=True)  13.5 us
    reshape x1, local copies, waits for them, and re-layouts, shards(): jnp.concatenate(lax.all_to_all(jnp.stack([w_qkv] * lax.axis_size(('req',...  10.6 us
  transfers between devices with their start and end apart: 11, of which 7 were waited for; matrix products, arithmetic and copies ran while one was open for 26% of the time, Pallas kernels for 0%

profile of v1, /device:TPU:1, one launch (start us, length us, event | category | flops | bytes accessed | tf_op | source)
XLA Modules:
  0.0 517.7 jit_solution(5686953158112002258)
XLA Ops:
  7.2 5.0 stack.2
  12.2 16.5 %all-to-all-start = ((bf16[256,4,3072]{2,1,0:T(4,128)(2,1)}), bf16[256,4,3072]{2,1,0:T(4,128)(2,1)}, u32[]{:S(2)}, u32[]{:S(2)}) async-start(bf16[256,4,3072]{2,1,0:T(4,128)(2,1)} %stack.2), calls=%async_computation | async-start | bytes 12582912 | tf_op jit(solution)/shard_map/all_to_all | solution.py:121
  32.8 126.6 %all-gather.15.cloned.1.call-done = bf16[256,4,1024]{2,1,0:T(4,128)(2,1)} async-done(((bf16[1,4,1024]{2,1,0:T(4,128)(2,1)}), bf16[256,4,1024]{2,1,0:T(4,128)(2,1)}) %all-gather.15.cloned.1.call-update) | async-done | bytes 2097168 | tf_op jit(solution)/shard_map/all_gather | solution.py:142
  159.4 3.9 reshape.227
  163.3 13.9 %all-to-all-done = bf16[256,4,3072]{2,1,0:T(4,128)(2,1)} async-done(((bf16[256,4,3072]{2,1,0:T(4,128)(2,1)}), bf16[256,4,3072]{2,1,0:T(4,128)(2,1)}, u32[]{:S(2)}, u32[]{:S(2)}) %all-to-all-start) | async-done | bytes 6291488 | tf_op jit(solution)/shard_map/all_to_all | solution.py:121
  177.2 10.6 %reshape.211 = bf16[1024,3072]{1,0:T(8,128)(2,1)} reshape(bf16[256,4,3072]{2,1,0:T(4,128)(2,1)} %all-to-all-done) | data formatting | bytes 12582912 | tf_op jit(solution)/shard_map/reshape | solution.py:120
  187.9 4.6 convolution_convert_fusion
  192.5 2.2 divide_multiply_fusion
  197.5 4.1 fusion.30
  201.6 2.2 convolution_multiply_fusion.5
  203.9 2.1 multiply_reduce_fusion.7
  208.6 2.0 convolution_multiply_fusion.4
  210.7 4.1 fusion.27
  214.8 1.7 multiply_reduce_fusion.5
  218.4 2.0 convolution_multiply_fusion.3
  220.4 4.1 fusion.24
  224.6 1.7 multiply_reduce_fusion.3
  227.3 2.0 convolution_multiply_fusion.2
  229.3 4.3 fusion.21
  233.7 1.7 multiply_reduce_fusion.1
  236.8 4.1 fusion.18
  241.0 2.0 convolution_multiply_fusion.1
  243.0 1.6 fusion.34
  244.6 2.4 multiply_add_fusion.2
  247.0 2.0 convolution_multiply_fusion
  249.0 4.2 fusion.15
  259.5 3.2 all-to-all-start.1
  263.0 2.0 pad_maximum_fusion
  265.0 2.5 copy.96
  267.4 1.8 gather_fusion
  269.2 13.5 %all-gather.7.cloned.1.call-done = bf16[1024,1024]{1,0:T(8,128)(2,1)} async-done(((bf16[256,1024]{1,0:T(8,128)(2,1)}), bf16[1024,1024]{1,0:T(8,128)(2,1)}) %all-gather.7.cloned.1.call-update) | async-done | bytes 2097168 | tf_op jit(solution)/shard_map/all_gather | solution.py:147
  282.8 5.3 %fusion.104 = f32[1024,704]{0,1:T(8,128)} fusion(bf16[1024,1024]{1,0:T(8,128)(2,1)} %all-gather.7.cloned.1.call-done, bf16[1024,704]{1,0:T(8,128)(2,1)} %all-gather.9.cloned.1.call-done), kind=kOutput, calls=%fused_computation.173 | convolution fusion | flops 1476395008 | bytes 6422528 | tf_op jit(solution)/shard_map/dot_general | solution.py:149
  288.1 73.4 %all-gather.11.cloned.1.call-done = bf16[1024,704]{1,0:T(8,128)(2,1)} async-done(((bf16[16,704]{1,0:T(8,128)(2,1)}), bf16[1024,704]{1,0:T(8,128)(2,1)}) %all-gather.11.cloned.1.call-update) | async-done | bytes 1441808 | tf_op jit(solution)/shard_map/all_gather | solution.py:156
  361.5 77.3 %all-gather.13.cloned.1.call-done = bf16[704,1024]{0,1:T(8,128)(2,1)} async-done(((bf16[704,16]{0,1:T(8,128)(2,1)}), bf16[704,1024]{0,1:T(8,128)(2,1)}) %all-gather.13.cloned.1.call-update) | async-done | bytes 1441808 | tf_op jit(solution)/shard_map/all_gather | solution.py:160
  438.8 8.2 %convolution_convert_fusion.3 = bf16[1024,1024]{1,0:T(8,128)(2,1)} fusion(bf16[704,1024]{0,1:T(8,128)(2,1)} %all-gather.13.cloned.1.call-done, f32[1024,704]{0,1:T(8,128)} %fusion.104, bf16[1024,1024]{1,0:T(8,128)(2,1)} %all-gather.7.cloned.1.call-done, bf16[1024,704]{1,0:T(8,128)(2,1)} %all-gather.11.cloned.1.call-done), kind=kOutput, calls=%fused_computation.16 | convolution fusion | flops 2958163968 | bytes 9961472 | tf_op jit(solution)/shard_map/dot_general | solution.py:162
  447.9 7.5 %multiply_add_fusion = f32[4,8,128,128]{3,2,1,0:T(8,128)} fusion(f32[4,8,128,128]{3,2,1,0:T(8,128)} %param.20, f32[4,8]{1,0:T(4,128)S(1)} %exp.47, f32[4,64,1,8,128]{4,3,2,1,0:T(8,128)} %copy-done.1, f32[4,64,8]{1,2,0:T(8,128)S(1)} %get-tuple-element.43, f32[4,64,1,8,128]{4,3,2,1,0:T(8,128)S(1)} %get-tuple-element.37, f32[4,64,8]{1,2,0:T(8,128)S(1)} %add_rsqrt_fusion), kind=kOutput, calls=%fused_computation.14 | convolution fusion | flops 404226048 | bytes 6307968 | tf_op jit(solution)/shard_map/bshi,bshj->bhij/dot_general | solution.py:86
  455.3 4.8 all-to-all-start.4
  460.1 4.9 fusion.11
  466.2 4.2 all-to-all-start.3
  470.5 4.7 multiply_add_fusion.1
  475.1 3.3 fusion.8
  479.7 8.5 %all-to-all-done.3 = bf16[4,8,128,128]{3,2,1,0:T(8,128)(2,1)} async-done(((bf16[4,8,128,128]{3,2,1,0:T(8,128)(2,1)}), bf16[4,8,128,128]{3,2,1,0:T(8,128)(2,1)}, u32[]{:S(2)}, u32[]{:S(2)}) %all-to-all-start.3) | async-done | bytes 1048608 | tf_op jit(solution)/shard_map/all_to_all | solution.py:188
  488.2 4.3 all-to-all-start.2
  494.3 2.1 fusion.39
  496.4 1.6 copy.101
  498.0 8.0 %all-to-all-done.2 = bf16[4,8,128,128]{3,2,1,0:T(8,128)(2,1)S(1)} async-done(((bf16[4,8,128,128]{3,2,1,0:T(8,128)(2,1)}), bf16[4,8,128,128]{3,2,1,0:T(8,128)(2,1)S(1)}, u32[]{:S(2)}, u32[]{:S(2)}) %all-to-all-start.2) | async-done | bytes 1048608 | tf_op jit(solution)/shard_map/all_to_all | solution.py:185
  506.9 1.6 copy.100
  508.5 2.0 fusion.38
  (111 shorter events, 26.2 us)
Async XLA Ops:
  12.2 18.1 %copy-start.11 = (bf16[4,3,3072]{2,0,1:T(4,128)(2,1)S(1)}, bf16[4,3,3072]{2,0,1:T(4,128)(2,1)}, u32[]{:S(2)}) copy-start(bf16[4,3,3072]{2,0,1:T(4,128)(2,1)} %param.21) | copy-start | bytes 221188
  12.2 18.2 %copy-start.13 = (bf16[1024,16]{0,1:T(8,128)(2,1)S(1)}, bf16[1024,16]{0,1:T(8,128)(2,1)}, u32[]{:S(2)}) copy-start(bf16[1024,16]{0,1:T(8,128)(2,1)} %param.25) | copy-start | bytes 98308
  12.2 18.2 %copy-start.18 = (f32[8]{0:T(128)S(1)}, f32[8]{0:T(128)}, u32[]{:S(2)}) copy-start(f32[8]{0:T(128)} %param.26) | copy-start | bytes 100
  12.2 18.2 %copy-start.9 = (bf16[4,64,1024]{2,1,0:T(8,128)(2,1)S(1)}, bf16[4,64,1024]{2,1,0:T(8,128)(2,1)}, u32[]{:S(2)}) copy-start(bf16[4,64,1024]{2,1,0:T(8,128)(2,1)} %param.17) | copy-start | bytes 1572868
  12.2 18.4 %copy-start.17 = (s32[4]{0:T(128)S(1)}, s32[4]{0:T(128)}, u32[]{:S(2)}) copy-start(s32[4]{0:T(128)} %param.18) | copy-start | bytes 52
  12.2 18.5 %copy-start.15 = (f32[1024]{0:T(1024)S(1)}, f32[1024]{0:T(1024)}, u32[]{:S(2)}) copy-start(f32[1024]{0:T(1024)} %param.29) | copy-start | bytes 12292
  12.2 165.0 %all-to-all-start = ((bf16[256,4,3072]{2,1,0:T(4,128)(2,1)}), bf16[256,4,3072]{2,1,0:T(4,128)(2,1)}, u32[]{:S(2)}, u32[]{:S(2)}) async-start(bf16[256,4,3072]{2,1,0:T(4,128)(2,1)} %stack.2), calls=%async_computation | async-start | bytes 12582912 | tf_op jit(solution)/shard_map/all_to_all | solution.py:121
  28.8 4.0 copy-start.12
  28.8 130.6 %all-gather.15.cloned.1.call-start = ((), (), s32[]{:S(2)}) async-start(), calls=%async_computation.11 | async-start | bytes 2105344 | tf_op jit(solution)/shard_map/all_gather | solution.py:142
  29.5 239.7 %all-gather.9.cloned.1.call-start = ((), (), s32[]{:S(2)}) async-start(), calls=%async_computation.7 | async-start | bytes 1597440 | tf_op jit(solution)/shard_map/all_gather | solution.py:151
  30.3 252.5 %all-gather.7.cloned.1.call-start = ((), (), s32[]{:S(2)}) async-start(), calls=%async_computation.6 | async-start | bytes 2621440 | tf_op jit(solution)/shard_map/all_gather | solution.py:147
  192.5 2.3 copy-start.3
  195.6 57.6 %copy-start.1 = (f32[4,64,1,8,128]{4,3,2,1,0:T(8,128)}, f32[4,64,1,8,128]{4,3,2,1,0:T(8,128)S(1)}, u32[]{:S(2)}) copy-start(f32[4,64,1,8,128]{4,3,2,1,0:T(8,128)S(1)} %get-tuple-element.36) | copy-start | bytes 3145732
  195.6 2.0 copy-start
  201.6 2.2 copy-start.14
  247.0 2.0 copy-start.2
  253.2 1.7 copy-start.8
  253.2 1.7 copy-start.10
  254.5 1.2 copy-start.4
  254.9 1.7 copy-start.16
  254.9 3.8 copy-start.19
  255.8 0.8 copy-start.6
  257.6 103.9 %all-gather.11.cloned.1.call-start = ((), (), s32[]{:S(2)}) async-start(), calls=%async_computation.8 | async-start | bytes 1597440 | tf_op jit(solution)/shard_map/all_gather | solution.py:156
  258.1 180.7 %all-gather.13.cloned.1.call-start = ((), (), s32[]{:S(2)}) async-start(), calls=%async_computation.9 | async-start | bytes 1597440 | tf_op jit(solution)/shard_map/all_gather | solution.py:160
  259.5 195.8 %all-to-all-start.1 = ((s32[4,1,1]{2,1,0:T(1,128)}), s32[4,1,1]{2,1,0:T(1,128)S(1)}, u32[]{:S(2)}, u32[]{:S(2)}) async-start(s32[4,1,1]{2,1,0:T(1,128)} %copy.89), calls=%async_computation.2 | async-start | bytes 4096 | tf_op jit(solution)/shard_map/all_to_all | solution.py:192
  262.8 245.7 %reduce-scatter.2.cloned.1.call-start = ((), (), s32[]{:S(2)}) async-start(), calls=%async_computation.10 | async-start | bytes 2621440 | tf_op jit(solution)/shard_map/reduce_scatter | solution.py:161
  455.3 10.9 %all-to-all-start.4 = ((bf16[4,3,3072]{2,1,0:T(4,128)(2,1)}), bf16[4,3,3072]{2,1,0:T(4,128)(2,1)S(1)}, u32[]{:S(2)}, u32[]{:S(2)}) async-start(bf16[4,3,3072]{2,1,0:T(4,128)(2,1)} %copy.97), calls=%async_computation.5 | async-start | bytes 196608 | tf_op jit(solution)/shard_map/all_to_all | solution.py:191
  466.2 22.0 %all-to-all-start.3 = ((bf16[4,8,128,128]{3,2,1,0:T(8,128)(2,1)}), bf16[4,8,128,128]{3,2,1,0:T(8,128)(2,1)}, u32[]{:S(2)}, u32[]{:S(2)}) async-start(bf16[4,8,128,128]{3,2,1,0:T(8,128)(2,1)} %copy.94), calls=%async_computation.4 | async-start | bytes 2097152 | tf_op jit(solution)/shard_map/all_to_all | solution.py:188
  478.5 14.1 %copy-start.5 = (bf16[4,64,8,128]{3,1,2,0:T(8,128)(2,1)S(1)}, bf16[4,64,8,128]{3,1,2,0:T(8,128)(2,1)}, u32[]{:S(2)}) copy-start(bf16[4,64,8,128]{3,1,2,0:T(8,128)(2,1)} %copy-done.4) | copy-start | bytes 1572868
  488.2 17.8 %all-to-all-start.2 = ((bf16[4,8,128,128]{3,2,1,0:T(8,128)(2,1)}), bf16[4,8,128,128]{3,2,1,0:T(8,128)(2,1)S(1)}, u32[]{:S(2)}, u32[]{:S(2)}) async-start(bf16[4,8,128,128]{3,2,1,0:T(8,128)(2,1)} %copy.91), calls=%async_computation.3 | async-start | bytes 2097152 | tf_op jit(solution)/shard_map/all_to_all | solution.py:185
  506.9 1.6 copy-start.7
Sparse Core Ops, SparseCore 0:
  33.3 126.0 all-gather.14
  162.7 75.3 all-gather.8
  257.7 25.0 all-gather.6
  285.9 75.5 all-gather.10
  364.6 74.1 all-gather.12
  447.1 34.4 reduce-scatter.1
